TPU v7x, 32 devices: a whole 2x2x4 slice. The times are simulated.
32 devices in a mesh: dp: 8 (over y, x, core), tensor: 4 (over z).
Axes of the slice: x: 2, y: 2, z: 4, core: 2. Of those that a mesh axis runs over, the one named last changes fastest.
Arguments:
- images: bfloat16 [8, 577, 1024], P('dp'), may hold values from -6 to 6
- valid_flags: int32 [8], P('dp'), may hold values from 0 to 1, as said below
- cotangent: bfloat16 [8, 577, 1024], P('dp'), may hold values from -6 to 6
- first_gain: float32 [1024], P('dp'), may hold values from 0.5 to 1.5
- first_shift: float32 [1024], P('dp'), may hold values from -1.75 to 1.75
- triple_weight: float32 [3, 1024, 1024], P(None, 'dp', 'tensor'), may hold values from -0.1875 to 0.1875
- pair_bias: float32 [2, 16, 64], P(None, 'tensor', 'dp'), may hold values from -1.75 to 1.75
- output_weight: float32 [1024, 1024], P('tensor', 'dp'), may hold values from -1.5 to 1.5
- output_bias: float32 [1024], P('dp'), may hold values from -1.75 to 1.75
- second_gain: float32 [1024], P('dp'), may hold values from 0.5 to 1.5
- second_shift: float32 [1024], P('dp'), may hold values from -1.75 to 1.75
- expand_weight: float32 [1024, 4096], P('dp', 'tensor'), may hold values from -1 to 1, as said below
- expand_bias: float32 [64, 64], P('tensor', 'dp'), may hold values from -1.75 to 1.75
- reduce_weight: float32 [4096, 1024], P('tensor', 'dp'), may hold values from -1 to 1, as said below
- reduce_bias: float32 [1024], P('dp'), may hold values from -1.75 to 1.75
- first_gain_mean: float32 [1024], P('dp'), may hold values from -6 to 6
- first_shift_mean: float32 [1024], P('dp'), may hold values from -6 to 6
- triple_weight_mean: float32 [3, 1024, 1024], P(None, 'dp', 'tensor'), may hold values from -6 to 6
- pair_bias_mean: float32 [2, 16, 64], P(None, 'tensor', 'dp'), may hold values from -6 to 6
- output_weight_mean: float32 [1024, 1024], P('tensor', 'dp'), may hold values from -6 to 6
- output_bias_mean: float32 [1024], P('dp'), may hold values from -6 to 6
- second_gain_mean: float32 [1024], P('dp'), may hold values from -6 to 6
- second_shift_mean: float32 [1024], P('dp'), may hold values from -6 to 6
- expand_weight_mean: float32 [1024, 4096], P('dp', 'tensor'), may hold values from -6 to 6
- expand_bias_mean: float32 [64, 64], P('tensor', 'dp'), may hold values from -6 to 6
- reduce_weight_mean: float32 [4096, 1024], P('tensor', 'dp'), may hold values from -6 to 6
- reduce_bias_mean: float32 [1024], P('dp'), may hold values from -6 to 6
- first_gain_square: float32 [1024], P('dp'), may hold values from 1 to 4
- first_shift_square: float32 [1024], P('dp'), may hold values from 1 to 4
- triple_weight_square: float32 [3, 1024, 1024], P(None, 'dp', 'tensor'), may hold values from 1 to 4
- pair_bias_square: float32 [2, 16, 64], P(None, 'tensor', 'dp'), may hold values from 1 to 4
- output_weight_square: float32 [1024, 1024], P('tensor', 'dp'), may hold values from 1 to 4
- output_bias_square: float32 [1024], P('dp'), may hold values from 1 to 4
- second_gain_square: float32 [1024], P('dp'), may hold values from 1 to 4
- second_shift_square: float32 [1024], P('dp'), may hold values from 1 to 4
- expand_weight_square: float32 [1024, 4096], P('dp', 'tensor'), may hold values from 1 to 4
- expand_bias_square: float32 [64, 64], P('tensor', 'dp'), may hold values from 1 to 4
- reduce_weight_square: float32 [4096, 1024], P('tensor', 'dp'), may hold values from 1 to 4
- reduce_bias_square: float32 [1024], P('dp'), may hold values from 1 to 4
Outputs:
- block_output: bfloat16 [8, 577, 1024], P('dp')
- input_grad: float32 [8, 577, 1024], P('dp')
- grad_norm: float32 [], replicated
- new_first_gain: float32 [1024], P('dp')
- mean_first_gain: float32 [1024], P('dp')
- square_first_gain: float32 [1024], P('dp')
- copy_first_gain: bfloat16 [1024], P('dp')
- new_first_shift: float32 [1024], P('dp')
- mean_first_shift: float32 [1024], P('dp')
- square_first_shift: float32 [1024], P('dp')
- copy_first_shift: bfloat16 [1024], P('dp')
- new_triple_weight: float32 [3, 1024, 1024], P(None, 'dp', 'tensor')
- mean_triple_weight: float32 [3, 1024, 1024], P(None, 'dp', 'tensor')
- square_triple_weight: float32 [3, 1024, 1024], P(None, 'dp', 'tensor')
- copy_triple_weight: bfloat16 [3, 1024, 1024], P(None, 'dp', 'tensor')
- new_pair_bias: float32 [2, 16, 64], P(None, 'tensor', 'dp')
- mean_pair_bias: float32 [2, 16, 64], P(None, 'tensor', 'dp')
- square_pair_bias: float32 [2, 16, 64], P(None, 'tensor', 'dp')
- copy_pair_bias: bfloat16 [2, 16, 64], P(None, 'tensor', 'dp')
- new_output_weight: float32 [1024, 1024], P('tensor', 'dp')
- mean_output_weight: float32 [1024, 1024], P('tensor', 'dp')
- square_output_weight: float32 [1024, 1024], P('tensor', 'dp')
- copy_output_weight: bfloat16 [1024, 1024], P('tensor', 'dp')
- new_output_bias: float32 [1024], P('dp')
- mean_output_bias: float32 [1024], P('dp')
- square_output_bias: float32 [1024], P('dp')
- copy_output_bias: bfloat16 [1024], P('dp')
- new_second_gain: float32 [1024], P('dp')
- mean_second_gain: float32 [1024], P('dp')
- square_second_gain: float32 [1024], P('dp')
- copy_second_gain: bfloat16 [1024], P('dp')
- new_second_shift: float32 [1024], P('dp')
- mean_second_shift: float32 [1024], P('dp')
- square_second_shift: float32 [1024], P('dp')
- copy_second_shift: bfloat16 [1024], P('dp')
- new_expand_weight: float32 [1024, 4096], P('dp', 'tensor')
- mean_expand_weight: float32 [1024, 4096], P('dp', 'tensor')
- square_expand_weight: float32 [1024, 4096], P('dp', 'tensor')
- copy_expand_weight: bfloat16 [1024, 4096], P('dp', 'tensor')
- new_expand_bias: float32 [64, 64], P('tensor', 'dp')
- mean_expand_bias: float32 [64, 64], P('tensor', 'dp')
- square_expand_bias: float32 [64, 64], P('tensor', 'dp')
- copy_expand_bias: bfloat16 [64, 64], P('tensor', 'dp')
- new_reduce_weight: float32 [4096, 1024], P('tensor', 'dp')
- mean_reduce_weight: float32 [4096, 1024], P('tensor', 'dp')
- square_reduce_weight: float32 [4096, 1024], P('tensor', 'dp')
- copy_reduce_weight: bfloat16 [4096, 1024], P('tensor', 'dp')
- new_reduce_bias: float32 [1024], P('dp')
- mean_reduce_bias: float32 [1024], P('dp')
- square_reduce_bias: float32 [1024], P('dp')
- copy_reduce_bias: bfloat16 [1024], P('dp')
Inputs may be any that keep to these rules, and one draw needn't show every extreme that they name: `valid_flags`: at least one image is blank; blank images may stand anywhere in the batch. `expand_weight`: a projection matrix with entries of order one over the root of 1024. `reduce_weight`: a projection matrix with entries of order one over the root of 4096.
All inputs are finite; a program needn't handle non-finite values.
Results may differ from a plain program's by a relative error of at most 0.012.
The roundings to bfloat16 on the way count: a program that leaves them out, or rounds other values in their place, can miss the bound.
Values may be sent and summed in bfloat16 or wider, within the bound.
A program may use at most 128 MiB of HBM per device.

v0:
```python
import math
import jax
import jax.numpy as jnp
from jax import lax
from jax.sharding import PartitionSpec as P

D = 1024
FF = 4096
shard_dims = (0, 0, 1, 2, 1, 0, 0, 0, 0, 1, 1, 0)
shared_terms = (1, 1, 0, 0, 0, 1, 1, 1, 0, 0, 0, 1)
rates = (0.2, 0.2, 0.03, 0.2, 0.03, 0.2, 0.2, 0.2, 0.03, 0.2, 0.03, 0.2)


def apply_layer_norm(input_row_block, norm_gain, norm_bias):
    center = jnp.mean(input_row_block, axis=-1, keepdims=True)
    centered_rows = input_row_block - center
    inverse_deviation = lax.rsqrt(
        jnp.mean(centered_rows * centered_rows, axis=-1, keepdims=True) + 1e-06
    )
    standardized_rows = centered_rows * inverse_deviation
    return (
        standardized_rows * norm_gain.astype(jnp.float32) + norm_bias.astype(jnp.float32),
        standardized_rows,
        inverse_deviation,
    )


def layer_norm_backward(incoming_gradient, standardized_rows, inverse_deviation, norm_gain):
    scaled_rows = incoming_gradient * norm_gain.astype(jnp.float32)
    return inverse_deviation * (
        scaled_rows
        - jnp.mean(scaled_rows, axis=-1, keepdims=True)
        - standardized_rows * jnp.mean(scaled_rows * standardized_rows, axis=-1, keepdims=True)
    )


def contract_rows(left, right):
    return lax.dot_general(
        left, right, (((0,), (0,)), ((), ())), preferred_element_type=jnp.float32
    )


def against(left, right):
    return lax.dot_general(
        left, right, (((1,), (1,)), ((), ())), preferred_element_type=jnp.float32
    )


def exact_gelu(values):
    return jax.nn.gelu(values, approximate=False)


def image_forward(parts):
    query, keys, values = parts
    factor = float(query.shape[2]) ** (-0.5)
    scores = jnp.einsum("qhd,khd->hqk", query, keys, preferred_element_type=jnp.float32) * factor
    top = jnp.max(scores, axis=-1, keepdims=True)
    totals = jnp.sum(jnp.exp(scores - top), axis=-1, keepdims=True)
    logsum = top + jnp.log(totals)
    probs = jnp.exp(scores - logsum).astype(jnp.bfloat16)
    mixed = jnp.einsum("hqk,khd->qhd", probs, values, preferred_element_type=jnp.float32)
    return (mixed.astype(jnp.bfloat16), logsum)


def image_backward(parts):
    query, keys, values, logsum, grad_mixed = parts
    factor = float(query.shape[2]) ** (-0.5)
    scores = jnp.einsum("qhd,khd->hqk", query, keys, preferred_element_type=jnp.float32) * factor
    probs = jnp.exp(scores - logsum)
    grad_probs = jnp.einsum("qhd,khd->hqk", grad_mixed, values, preferred_element_type=jnp.float32)
    grad_scores = probs * (grad_probs - jnp.sum(probs * grad_probs, axis=-1, keepdims=True))
    rounded = grad_scores.astype(jnp.bfloat16)
    grad_query = (
        jnp.einsum("hqk,khd->qhd", rounded, keys, preferred_element_type=jnp.float32) * factor
    )
    grad_keys = (
        jnp.einsum("hqk,qhd->khd", rounded, query, preferred_element_type=jnp.float32) * factor
    )
    grad_values = jnp.einsum(
        "hqk,qhd->khd", probs.astype(jnp.bfloat16), grad_mixed, preferred_element_type=jnp.float32
    )
    return (
        grad_query.astype(jnp.bfloat16),
        grad_keys.astype(jnp.bfloat16),
        grad_values.astype(jnp.bfloat16),
    )


def squared_total(grads, tensor_count):
    total = jnp.zeros((), jnp.float32)
    for incoming_gradient, shared in zip(grads, shared_terms):
        weight = 1.0 / tensor_count if shared else 1.0
        total = total + weight * jnp.sum(incoming_gradient * incoming_gradient)
    return total


def adam_step(master, row_mean, square, incoming_gradient, rate):
    mean_new = 0.5 * row_mean + 0.5 * incoming_gradient
    square_new = 0.5 * square + 0.5 * incoming_gradient * incoming_gradient
    change = -rate * (mean_new / (jnp.sqrt(square_new) + 1e-08) + 0.1 * master)
    updated = master + change
    return [updated, mean_new, square_new, updated.astype(jnp.bfloat16)]


def per_device(
    images,
    valid_flags,
    cotangent,
    first_gain,
    first_shift,
    triple_weight,
    pair_bias,
    output_weight,
    output_bias,
    second_gain,
    second_shift,
    expand_weight,
    expand_bias,
    reduce_weight,
    reduce_bias,
    first_gain_mean,
    first_shift_mean,
    triple_weight_mean,
    pair_bias_mean,
    output_weight_mean,
    output_bias_mean,
    second_gain_mean,
    second_shift_mean,
    expand_weight_mean,
    expand_bias_mean,
    reduce_weight_mean,
    reduce_bias_mean,
    first_gain_square,
    first_shift_square,
    triple_weight_square,
    pair_bias_square,
    output_weight_square,
    output_bias_square,
    second_gain_square,
    second_shift_square,
    expand_weight_square,
    expand_bias_square,
    reduce_weight_square,
    reduce_bias_square,
):
    masters = (
        first_gain,
        first_shift,
        triple_weight,
        pair_bias,
        output_weight,
        output_bias,
        second_gain,
        second_shift,
        expand_weight,
        expand_bias,
        reduce_weight,
        reduce_bias,
    )
    means = (
        first_gain_mean,
        first_shift_mean,
        triple_weight_mean,
        pair_bias_mean,
        output_weight_mean,
        output_bias_mean,
        second_gain_mean,
        second_shift_mean,
        expand_weight_mean,
        expand_bias_mean,
        reduce_weight_mean,
        reduce_bias_mean,
    )
    squares = (
        first_gain_square,
        first_shift_square,
        triple_weight_square,
        pair_bias_square,
        output_weight_square,
        output_bias_square,
        second_gain_square,
        second_shift_square,
        expand_weight_square,
        expand_bias_square,
        reduce_weight_square,
        reduce_bias_square,
    )
    rounded = tuple((master.astype(jnp.bfloat16) for master in masters))
    (
        first_norm_gain,
        first_norm_bias,
        triple,
        pairs,
        out_weight,
        out_bias,
        second_norm_gain,
        second_norm_bias,
        up_weight,
        up_bias,
        down_weight,
        down_bias,
    ) = (
        lax.all_gather(rounded[0], "dp", axis=0, tiled=True),
        lax.all_gather(rounded[1], "dp", axis=0, tiled=True),
        lax.all_gather(rounded[2], "dp", axis=1, tiled=True),
        lax.all_gather(rounded[3], "dp", axis=2, tiled=True),
        lax.all_gather(rounded[4], "dp", axis=1, tiled=True),
        lax.all_gather(rounded[5], "dp", axis=0, tiled=True),
        lax.all_gather(rounded[6], "dp", axis=0, tiled=True),
        lax.all_gather(rounded[7], "dp", axis=0, tiled=True),
        lax.all_gather(rounded[8], "dp", axis=0, tiled=True),
        lax.all_gather(rounded[9], "dp", axis=1, tiled=True),
        lax.all_gather(rounded[10], "dp", axis=1, tiled=True),
        lax.all_gather(rounded[11], "dp", axis=0, tiled=True),
    )
    shape = images.shape
    count = shape[0] * shape[1]
    heads_local = pairs.shape[1]
    head_size = pairs.shape[2]
    split = (shape[0], shape[1], heads_local, head_size)
    tensor_count = lax.axis_size("tensor")
    input_row_block = images.reshape(count, shape[2]).astype(jnp.float32)
    first_normed_rows, first_standardized, first_inverse_deviation = apply_layer_norm(
        input_row_block, first_norm_gain, first_norm_bias
    )
    inputs_one = first_normed_rows.astype(jnp.bfloat16)
    projected = jnp.einsum("td,cde->cte", inputs_one, triple, preferred_element_type=jnp.float32)
    pair_flat = pairs.reshape(2, -1).astype(jnp.float32)
    query = (projected[0] + pair_flat[0]).astype(jnp.bfloat16).reshape(split)
    keys = projected[1].astype(jnp.bfloat16).reshape(split)
    values = (projected[2] + pair_flat[1]).astype(jnp.bfloat16).reshape(split)
    mixed, logsum = lax.map(image_forward, (query, keys, values))
    mixed_flat = mixed.reshape(count, -1)
    attn_part = jnp.dot(mixed_flat, out_weight, preferred_element_type=jnp.float32)
    middle_state = input_row_block + lax.psum(attn_part, "tensor") + out_bias.astype(jnp.float32)
    second_normed_rows, second_standardized, second_inverse_deviation = apply_layer_norm(
        middle_state, second_norm_gain, second_norm_bias
    )
    inputs_two = second_normed_rows.astype(jnp.bfloat16)
    hidden = jnp.dot(inputs_two, up_weight, preferred_element_type=jnp.float32) + up_bias.reshape(
        -1
    ).astype(jnp.float32)
    active_full, gelu_back = jax.vjp(exact_gelu, hidden)
    active = active_full.astype(jnp.bfloat16)
    mlp_part = jnp.dot(active, down_weight, preferred_element_type=jnp.float32)
    result = middle_state + lax.psum(mlp_part, "tensor") + down_bias.astype(jnp.float32)
    block_output = result.astype(jnp.bfloat16)
    output_gradient = (
        cotangent.astype(jnp.float32) * valid_flags.astype(jnp.float32)[:, None, None]
    ).reshape(count, -1)
    grad_low = output_gradient.astype(jnp.bfloat16)
    grad_down_bias = jnp.sum(output_gradient, axis=0)
    grad_down_weight = contract_rows(active, grad_low)
    grad_active = against(grad_low, down_weight)
    grad_hidden = gelu_back(grad_active)[0]
    grad_up_bias = jnp.sum(grad_hidden, axis=0).reshape(up_bias.shape)
    hidden_low = grad_hidden.astype(jnp.bfloat16)
    grad_up_weight = contract_rows(inputs_two, hidden_low)
    second_normed_gradient = lax.psum(against(hidden_low, up_weight), "tensor")
    second_gain_gradient = jnp.sum(second_normed_gradient * second_standardized, axis=0)
    grad_shift_two = jnp.sum(second_normed_gradient, axis=0)
    middle_gradient = output_gradient + layer_norm_backward(
        second_normed_gradient, second_standardized, second_inverse_deviation, second_norm_gain
    )
    grad_out_bias = jnp.sum(middle_gradient, axis=0)
    middle_low = middle_gradient.astype(jnp.bfloat16)
    grad_out_weight = contract_rows(mixed_flat, middle_low)
    grad_mixed = against(middle_low, out_weight).astype(jnp.bfloat16).reshape(split)
    grad_query, grad_keys, grad_values = lax.map(
        image_backward, (query, keys, values, logsum, grad_mixed)
    )
    stacked = jnp.stack(
        [
            grad_query.reshape(count, -1),
            grad_keys.reshape(count, -1),
            grad_values.reshape(count, -1),
        ]
    )
    grad_pairs = jnp.stack(
        [
            jnp.sum(stacked[0].astype(jnp.float32), axis=0),
            jnp.sum(stacked[2].astype(jnp.float32), axis=0),
        ]
    ).reshape(pairs.shape)
    grad_triple = jnp.einsum("td,cte->cde", inputs_one, stacked, preferred_element_type=jnp.float32)
    back_one = jnp.einsum("cte,cde->td", stacked, triple, preferred_element_type=jnp.float32)
    first_normed_gradient = lax.psum(back_one, "tensor")
    first_gain_gradient = jnp.sum(first_normed_gradient * first_standardized, axis=0)
    grad_shift_one = jnp.sum(first_normed_gradient, axis=0)
    row_gradient = middle_gradient + layer_norm_backward(
        first_normed_gradient, first_standardized, first_inverse_deviation, first_norm_gain
    )
    grads = (
        first_gain_gradient,
        grad_shift_one,
        grad_triple,
        grad_pairs,
        grad_out_weight,
        grad_out_bias,
        second_gain_gradient,
        grad_shift_two,
        grad_up_weight,
        grad_up_bias,
        grad_down_weight,
        grad_down_bias,
    )
    summed = lax.psum(
        (
            grads[0],
            grads[1],
            grads[2],
            grads[3],
            grads[4],
            grads[5],
            grads[6],
            grads[7],
            grads[8],
            grads[9],
            grads[10],
            grads[11],
        ),
        "dp",
    )
    total = lax.psum(squared_total(summed, tensor_count), "tensor")
    position = lax.axis_index("dp")
    owned = tuple(
        (
            lax.dynamic_slice_in_dim(
                incoming_gradient, position * master.shape[dim], master.shape[dim], dim
            )
            for incoming_gradient, master, dim in zip(summed, masters, shard_dims)
        )
    )
    norm_value = jnp.sqrt(total)
    limit = math.sqrt(4 * D * D + 2 * D * FF + 8 * D + FF)
    factor = jnp.minimum(1.0, limit / (norm_value + 1e-06))
    updates = []
    for master, row_mean, square, incoming_gradient, rate in zip(
        masters, means, squares, owned, rates
    ):
        updates.extend(adam_step(master, row_mean, square, incoming_gradient * factor, rate))
    return (block_output.reshape(shape), row_gradient.reshape(shape), norm_value, *updates)


def solution(mesh):
    in_specs = (
        P("dp", None, None),
        P("dp"),
        P("dp", None, None),
        P("dp"),
        P("dp"),
        P(None, "dp", "tensor"),
        P(None, "tensor", "dp"),
        P("tensor", "dp"),
        P("dp"),
        P("dp"),
        P("dp"),
        P("dp", "tensor"),
        P("tensor", "dp"),
        P("tensor", "dp"),
        P("dp"),
        P("dp"),
        P("dp"),
        P(None, "dp", "tensor"),
        P(None, "tensor", "dp"),
        P("tensor", "dp"),
        P("dp"),
        P("dp"),
        P("dp"),
        P("dp", "tensor"),
        P("tensor", "dp"),
        P("tensor", "dp"),
        P("dp"),
        P("dp"),
        P("dp"),
        P(None, "dp", "tensor"),
        P(None, "tensor", "dp"),
        P("tensor", "dp"),
        P("dp"),
        P("dp"),
        P("dp"),
        P("dp", "tensor"),
        P("tensor", "dp"),
        P("tensor", "dp"),
        P("dp"),
    )
    out_specs = (
        P("dp", None, None),
        P("dp", None, None),
        P(),
        P("dp"),
        P("dp"),
        P("dp"),
        P("dp"),
        P("dp"),
        P("dp"),
        P("dp"),
        P("dp"),
        P(None, "dp", "tensor"),
        P(None, "dp", "tensor"),
        P(None, "dp", "tensor"),
        P(None, "dp", "tensor"),
        P(None, "tensor", "dp"),
        P(None, "tensor", "dp"),
        P(None, "tensor", "dp"),
        P(None, "tensor", "dp"),
        P("tensor", "dp"),
        P("tensor", "dp"),
        P("tensor", "dp"),
        P("tensor", "dp"),
        P("dp"),
        P("dp"),
        P("dp"),
        P("dp"),
        P("dp"),
        P("dp"),
        P("dp"),
        P("dp"),
        P("dp"),
        P("dp"),
        P("dp"),
        P("dp"),
        P("dp", "tensor"),
        P("dp", "tensor"),
        P("dp", "tensor"),
        P("dp", "tensor"),
        P("tensor", "dp"),
        P("tensor", "dp"),
        P("tensor", "dp"),
        P("tensor", "dp"),
        P("tensor", "dp"),
        P("tensor", "dp"),
        P("tensor", "dp"),
        P("tensor", "dp"),
        P("dp"),
        P("dp"),
        P("dp"),
        P("dp"),
    )
    return jax.shard_map(
        per_device, mesh=mesh, in_specs=in_specs, out_specs=out_specs, check_vma=False
    )
```

profile of v0, /device:TPU:0, one launch (start us, length us, event | category | flops | bytes accessed | tf_op | source)
XLA Modules:
  0.0 777.6 jit_solution(4180550084816320558)
XLA Ops:
  9.8 10.3 %all-gather.1 = bf16[8,1,128]{2,1,0:T(2,128)(2,1)S(1)} all-gather(bf16[1,1,128]{2,1,0:T(2,128)(2,1)S(1)} %convert_bitcast_fusion.5), channel_id=1, replica_groups=mesh['dp'=8,'tensor'=4] {'dp'}, dimensions={0}, use_global_device_ids=true | all-gather | bytes 2304 | tf_op jit(solution)/shard_map/all_gather | solution.py:204
  20.7 8.8 %all-gather = bf16[8,1,128]{2,1,0:T(2,128)(2,1)S(1)} all-gather(bf16[1,1,128]{2,1,0:T(2,128)(2,1)S(1)} %convert_bitcast_fusion.6), channel_id=1, replica_groups=mesh['dp'=8,'tensor'=4] {'dp'}, dimensions={0}, use_global_device_ids=true | all-gather | bytes 2304 | tf_op jit(solution)/shard_map/all_gather | solution.py:203
  30.3 8.1 %all_gather.39 = bf16[2,4,64]{1,0,2:T(2,128)(2,1)S(1)} all-gather(bf16[2,4,8]{1,0,2:T(2,128)(2,1)S(1)} %copy.199), channel_id=1, replica_groups=mesh['dp'=8,'tensor'=4] {'dp'}, dimensions={2}, use_global_device_ids=true | all-gather | bytes 1152 | tf_op jit(solution)/shard_map/all_gather | solution.py:206
  39.5 10.1 %all_gather.40 = bf16[256,1024]{1,0:T(8,128)(2,1)S(1)} all-gather(bf16[256,128]{1,0:T(8,128)(2,1)S(1)} %convert_element_type.217), channel_id=1, replica_groups=mesh['dp'=8,'tensor'=4] {'dp'}, dimensions={1}, use_global_device_ids=true | all-gather | bytes 589824 | tf_op jit(solution)/shard_map/all_gather | solution.py:207
  50.4 2.8 convolution_bitcast_fusion.2
  57.8 3.9 convolution_convert_fusion.1
  61.8 2.0 fusion.93
  65.6 7.8 %all-gather.2 = bf16[8,1,128]{2,1,0:T(2,128)(2,1)S(1)} all-gather(bf16[1,1,128]{2,1,0:T(2,128)(2,1)S(1)} %convert_bitcast_fusion.4), channel_id=1, replica_groups=mesh['dp'=8,'tensor'=4] {'dp'}, dimensions={0}, use_global_device_ids=true | all-gather | bytes 2304 | tf_op jit(solution)/shard_map/all_gather | solution.py:208
  73.5 8.9 %all_gather.45 = bf16[16,64]{0,1:T(8,128)(2,1)S(1)} all-gather(bf16[16,8]{0,1:T(8,128)(2,1)S(1)} %convert_element_type.226), channel_id=1, replica_groups=mesh['dp'=8,'tensor'=4] {'dp'}, dimensions={1}, use_global_device_ids=true | all-gather | bytes 2304 | tf_op jit(solution)/shard_map/all_gather | solution.py:212
  82.5 7.8 %all-gather.4 = bf16[8,1,128]{2,1,0:T(2,128)(2,1)S(1)} all-gather(bf16[1,1,128]{2,1,0:T(2,128)(2,1)S(1)} %convert_bitcast_fusion.2), channel_id=1, replica_groups=mesh['dp'=8,'tensor'=4] {'dp'}, dimensions={0}, use_global_device_ids=true | all-gather | bytes 2304 | tf_op jit(solution)/shard_map/all_gather | solution.py:210
  90.3 9.2 %all-gather.3 = bf16[8,1,128]{2,1,0:T(2,128)(2,1)S(1)} all-gather(bf16[1,1,128]{2,1,0:T(2,128)(2,1)S(1)} %convert_bitcast_fusion.3), channel_id=1, replica_groups=mesh['dp'=8,'tensor'=4] {'dp'}, dimensions={0}, use_global_device_ids=true | all-gather | bytes 2304 | tf_op jit(solution)/shard_map/all_gather | solution.py:209
  100.2 59.8 %all-reduce.8.cloned.1.call-done = f32[577,1024]{1,0:T(8,128)} async-done(((f32[577,1024]{1,0:T(8,128)}), f32[577,1024]{1,0:T(8,128)}) %all-reduce.8.cloned.1.call-update) | async-done | bytes 2363408 | tf_op jit(solution)/shard_map/psum | solution.py:235
  160.0 2.4 fusion.88
  162.8 26.4 %all-gather.12.cloned.1.call-done = bf16[1024,1024]{1,0:T(8,128)(2,1)} async-done(((bf16[128,1024]{1,0:T(8,128)(2,1)}), bf16[1024,1024]{1,0:T(8,128)(2,1)}) %all-gather.12.cloned.1.call-update) | async-done | bytes 2097168 | tf_op jit(solution)/shard_map/all_gather | solution.py:211
  189.2 10.2 %multiply_convert_fusion.1 = (bf16[577,1024]{1,0:T(8,128)(2,1)}, f32[577,1024]{1,0:T(8,128)}, f32[577,1024]{1,0:T(8,128)}) fusion(f32[1024]{0:T(1024)S(1)} %reshape.236, bf16[1024,1024]{1,0:T(8,128)(2,1)} %all-gather.12.cloned.1.call-done, f32[577,1024]{1,0:T(8,128)S(1)} %get-tuple-element.426, f32[1024]{0:T(1024)S(1)} %bitcast.159, ...), kind=kOutput, calls=%fused_computation.39 | convolution fusion | flops 1252006912 | bytes 10385928 | tf_op jit(solution)/shard_map/dot_general | solution.py:240
  199.4 20.3 %all-gather.14.cloned.1.call-done = bf16[1024,1024]{1,0:T(8,128)(2,1)} async-done(((bf16[1024,128]{1,0:T(8,128)(2,1)}), bf16[1024,1024]{1,0:T(8,128)(2,1)}) %all-gather.14.cloned.1.call-update) | async-done | bytes 2097168 | tf_op jit(solution)/shard_map/all_gather | solution.py:213
  219.7 5.7 fusion.92
  226.4 2.9 fusion.37
  229.6 4.9 fusion.94
  234.5 90.8 %all-reduce.10.cloned.1.call-done = f32[577,1024]{1,0:T(8,128)} async-done(((f32[577,1024]{1,0:T(8,128)}), f32[577,1024]{1,0:T(8,128)}) %all-reduce.10.cloned.1.call-update) | async-done | bytes 2363408 | tf_op jit(solution)/shard_map/psum | solution.py:259
  325.3 2.8 multiply_reduce_fusion.5
  331.9 1.9 copy.206
  333.7 4.8 convert_reduce_fusion.1
  338.6 4.4 multiply_reduce_fusion
  348.9 1.8 copy.210
  350.7 4.0 convolution_bitcast_fusion.1
  355.1 5.7 fusion.30
  360.8 4.1 fusion.35
  366.5 3.5 convolution_bitcast_fusion
  372.3 1.9 copy.214
  375.9 152.1 %all-reduce.14.cloned.1.call-done = (f32[577,1024]{1,0:T(8,128)}, f32[577,1024]{1,0:T(8,128)}) async-done(((f32[577,1024]{1,0:T(8,128)}, f32[577,1024]{1,0:T(8,128)}), (f32[577,1024]{1,0:T(8,128)}, f32[577,1024]{1,0:T(8,128)})) %all-reduce.14.cloned.1.call-update) | async-done | bytes 4726800 | tf_op jit(solution)/shard_map/psum | solution.py:246
  528.0 3.0 fusion.16
  531.1 26.5 %all-reduce = (f32[1024]{0:T(1024)S(1)}, f32[1024]{0:T(1024)S(1)}, f32[2,4,64]{2,1,0:T(4,128)S(1)}, f32[1024]{0:T(1024)S(1)}, f32[1024]{0:T(1024)S(1)}, /*index=...) all-reduce(f32[1024]{0:T(1024)S(1)} %get-tuple-element.353, ...), channel_id=1, replica_groups=mesh['dp'=8,'tensor'=4] {'dp'}, use_global_device_ids=true, to_apply=%region_16.17 | all-reduce | flops 7680 | bytes 61440 | tf_op jit(solution)/shard_map/psum | solution.py:307
  566.4 5.5 fusion.15
  571.8 132.6 %all-reduce.12.cloned.1.call-done = (f32[3,1024,256]{1,2,0:T(8,128)}, f32[256,1024]{1,0:T(8,128)}, f32[1024,1024]{1,0:T(8,128)}, f32[1024,1024]{1,0:T(8,128)}) async-done(((f32[3,1024,256]{1,2,0:T(8,128)}, f32[256,1024]{1,0:T(8,128)}, f32[1024,1024]{1,0:T(8,128)}, f32[1024,1024]{1,0:T(8,128)}), (f32[3,1024,256]{1,2,0:T(8,128)}, f32[256,1024]{1,0:T(8,128)}, f32[1024,1024]{1,0:T(8,128)}, ...) | async-done | bytes 12582928 | tf_op jit(solution)/shard_map/psum | solution.py:307
  704.5 3.5 multiply_reduce_fusion.4
  707.9 2.2 multiply_reduce_fusion.10
  717.5 5.5 copy.218
  723.0 12.2 %psum.135 = f32[]{:T(128)} all-reduce(f32[]{:T(128)S(6)} %add.421), channel_id=1, replica_groups=mesh['dp'=8,'tensor'=4] {'tensor'}, use_global_device_ids=true, to_apply=%region_48.49 | all-reduce | flops 1 | bytes 8 | tf_op jit(solution)/shard_map/psum | solution.py:324
  736.5 8.7 %all-gather.5 = bf16[8,1,128]{2,1,0:T(2,128)(2,1)S(1)} all-gather(bf16[1,1,128]{2,1,0:T(2,128)(2,1)S(1)} %get-tuple-element.431), channel_id=1, replica_groups=mesh['dp'=8,'tensor'=4] {'dp'}, dimensions={0}, use_global_device_ids=true | all-gather | bytes 2304 | tf_op jit(solution)/shard_map/all_gather | solution.py:214
  745.3 2.3 fusion.80
  747.6 1.9 copy.219
  749.5 1.9 copy.220
  751.4 1.9 copy.221
  754.3 3.5 fusion.28
  759.2 1.8 fusion.76
  762.9 2.6 fusion.68
  766.8 2.6 fusion.64
  (208 shorter events, 43.6 us)
Async XLA Ops:
  7.2 42.4 %copy-start.3 = (bf16[1,577,1024]{2,1,0:T(8,128)(2,1)S(1)}, bf16[1,577,1024]{2,1,0:T(8,128)(2,1)}, u32[]{:S(2)}) copy-start(bf16[1,577,1024]{2,1,0:T(8,128)(2,1)} %param.39) | copy-start | bytes 3545092
  7.3 43.2 %all-gather.10.cloned.1.call-start = ((), (), s32[]{:S(2)}) async-start(), calls=%async_computation | async-start | bytes 1769472 | tf_op jit(solution)/shard_map/all_gather | solution.py:205
  9.1 150.9 %all-reduce.8.cloned.1.call-start = ((), (), s32[]{:S(2)}) async-start(), calls=%async_computation.1 | async-start | bytes 4784128 | tf_op jit(solution)/shard_map/psum | solution.py:235
  49.7 12.1 %copy-start.11 = (bf16[256,1024]{1,0:T(8,128)(2,1)}, bf16[256,1024]{1,0:T(8,128)(2,1)S(1)}, u32[]{:S(2)}) copy-start(bf16[256,1024]{1,0:T(8,128)(2,1)S(1)} %all_gather.40) | copy-start | bytes 1572868
  63.8 9.7 %copy-start.31 = (f32[16,8]{0,1:T(8,128)S(1)}, f32[16,8]{0,1:T(8,128)}, u32[]{:S(2)}) copy-start(f32[16,8]{0,1:T(8,128)} %param.51) | copy-start | bytes 1540
  63.8 18.7 %copy-start.48 = (f32[128]{0:T(128)S(1)}, f32[128]{0:T(128)}, u32[]{:S(2)}) copy-start(f32[128]{0:T(128)} %param.49) | copy-start | bytes 1540
  63.8 26.6 %copy-start.45 = (f32[128]{0:T(128)S(1)}, f32[128]{0:T(128)}, u32[]{:S(2)}) copy-start(f32[128]{0:T(128)} %param.48) | copy-start | bytes 1540
  63.8 125.4 %all-gather.12.cloned.1.call-start = ((), (), s32[]{:S(2)}) async-start(), calls=%async_computation.2 | async-start | bytes 2359296 | tf_op jit(solution)/shard_map/all_gather | solution.py:211
  64.6 155.1 %all-gather.14.cloned.1.call-start = ((), (), s32[]{:S(2)}) async-start(), calls=%async_computation.3 | async-start | bytes 2359296 | tf_op jit(solution)/shard_map/all_gather | solution.py:213
  65.6 259.8 %all-reduce.10.cloned.1.call-start = ((), (), s32[]{:S(2)}) async-start(), calls=%async_computation.4 | async-start | bytes 4784128 | tf_op jit(solution)/shard_map/psum | solution.py:259
  219.7 6.8 copy-start.54
  229.4 298.7 %all-reduce.14.cloned.1.call-start = ((), (), s32[]{:S(2)}) async-start(), calls=%async_computation.6 | async-start | bytes 9568256 | tf_op jit(solution)/shard_map/psum | solution.py:246
  333.7 4.8 copy-start.13
  333.7 9.3 %slice-start = ((s8[5980160]{0:T(1024)(128)(4,1)}), s8[4194304]{0:T(1024)(128)(4,1)S(1)}, s32[]{:S(2)}) async-start(s8[5980160]{0:T(1024)(128)(4,1)} %bitcast.128), calls=%async_computation.7 | async-start | bytes 8388608
  338.6 4.4 slice-start.1
  354.8 349.7 %all-reduce.12.cloned.1.call-start = ((), (), s32[]{:S(2)}) async-start(), calls=%async_computation.5 | async-start | bytes 25165824 | tf_op jit(solution)/shard_map/psum | solution.py:307
  355.1 5.7 copy-start.56
  360.8 4.1 copy-start.2
  704.5 5.7 copy-start.9
  707.9 3.9 copy-start.8
  713.5 22.4 %copy-start.51 = (f32[128]{0:T(128)S(1)}, f32[128]{0:T(128)}, u32[]{:S(2)}) copy-start(f32[128]{0:T(128)} %param.53) | copy-start | bytes 1540
  713.5 22.4 %copy-start.52 = (f32[128]{0:T(128)S(1)}, f32[128]{0:T(128)}, u32[]{:S(2)}) copy-start(f32[128]{0:T(128)} %param.77) | copy-start | bytes 1540
  713.5 22.4 %copy-start.53 = (f32[128]{0:T(128)S(1)}, f32[128]{0:T(128)}, u32[]{:S(2)}) copy-start(f32[128]{0:T(128)} %param.65) | copy-start | bytes 1540
  754.2 3.7 copy-start.37
  754.2 3.7 copy-start.38
  754.2 4.3 copy-start.39
  754.2 4.3 copy-start.40
  754.2 4.3 copy-start.41
  754.2 4.9 copy-start.26
  754.2 4.9 copy-start.28
  754.2 4.9 copy-start.29
  754.2 6.8 copy-start.43
  754.2 6.8 copy-start.44
  754.2 7.4 copy-start.46
  754.3 7.4 copy-start.47
  754.3 8.0 %copy-start.49 = (f32[128]{0:T(128)S(1)}, f32[128]{0:T(128)}, u32[]{:S(2)}) copy-start(f32[128]{0:T(128)} %param.73) | copy-start | bytes 1540
  754.3 8.0 %copy-start.50 = (f32[128]{0:T(128)S(1)}, f32[128]{0:T(128)}, u32[]{:S(2)}) copy-start(f32[128]{0:T(128)} %param.61) | copy-start | bytes 1540
  754.3 8.6 %copy-start.17 = (f32[128,1024]{1,0:T(8,128)S(1)}, f32[128,1024]{1,0:T(8,128)}, u32[]{:S(2)}) copy-start(f32[128,1024]{1,0:T(8,128)} %param.50) | copy-start | bytes 1572868
  754.3 8.6 %copy-start.22 = (f32[128,1024]{1,0:T(8,128)S(1)}, f32[128,1024]{1,0:T(8,128)}, u32[]{:S(2)}) copy-start(f32[128,1024]{1,0:T(8,128)} %param.74) | copy-start | bytes 1572868
  754.3 8.6 %copy-start.23 = (f32[128,1024]{1,0:T(8,128)S(1)}, f32[128,1024]{1,0:T(8,128)}, u32[]{:S(2)}) copy-start(f32[128,1024]{1,0:T(8,128)} %param.62) | copy-start | bytes 1572868
  759.1 6.4 copy-start.30
  759.1 6.4 copy-start.32
  759.1 6.3 copy-start.33
  759.1 7.0 copy-start.34
  759.2 7.0 copy-start.35
  759.2 7.6 copy-start.19
  759.2 7.6 copy-start.24
  759.2 7.6 copy-start.25
  (18 other events, 33.3 us)
Sparse Core Ops, SparseCore 0:
  10.5 28.3 all-gather.9
  63.9 96.0 all-reduce.7
  162.5 26.7 all-gather.11
  191.5 28.0 all-gather.13
  229.5 95.7 all-reduce.9
  354.9 173.0 all-reduce.13
  532.6 171.8 all-reduce.11
where the time goes:
time: 785 us; the launch traced here: 778 us
  waiting for transfers between devices  482 us (61%)
  blocking collectives  118 us (15%)
  matrix products  66.1 us (8%)
  other arithmetic  57.7 us (7%)
  local copies, waits for them, and re-layouts  27 us (3%)
  between operations  25.5 us (3%)
    psum x1, waiting for transfers between devices, per_device(): lax.psum(mlp_part, 'tensor')  152 us
    psum x1, waiting for transfers between devices, per_device(): lax.psum((grads[0], grads[1], grads[2], grads[3], grads[4], grads[5], gra...  133 us
    psum x1, waiting for transfers between devices, per_device(): second_normed_gradient = lax.psum(against(hidden_low, up_weight), 'tensor')  90.8 us
    psum x1, waiting for transfers between devices, per_device(): lax.psum(attn_part, 'tensor')  59.8 us
    psum x1, blocking collectives, per_device(): lax.psum((grads[0], grads[1], grads[2], grads[3], grads[4], grads[5], gra...  26.5 us
    all_gather x1, waiting for transfers between devices, per_device(): lax.all_gather(rounded[8], 'dp', axis=0, tiled=True)  26.4 us
    unnamed x126, local copies, waits for them, and re-layouts  20.7 us
    all_gather x1, waiting for transfers between devices, per_device(): lax.all_gather(rounded[10], 'dp', axis=1, tiled=True)  20.3 us
  transfers between devices with their start and end apart: 7, of which 6 were waited for; matrix products, arithmetic and copies ran while one was open for 7% of the time, Pallas kernels for 0%

commit v1 on v0

--- a/solution.py
+++ b/solution.py
@@ -1,3 +1,4 @@
+import functools
 import math
 import jax
 import jax.numpy as jnp
@@ -9,6 +10,14 @@
 shard_dims = (0, 0, 1, 2, 1, 0, 0, 0, 0, 1, 1, 0)
 shared_terms = (1, 1, 0, 0, 0, 1, 1, 1, 0, 0, 0, 1)
 rates = (0.2, 0.2, 0.03, 0.2, 0.03, 0.2, 0.2, 0.2, 0.03, 0.2, 0.03, 0.2)
+
+
+def _arrange_hubs(vals, ax_name):
+    passed = lax.all_gather(vals, ax_name)
+    return jnp.sum(passed, axis=0)
+
+
+put_group = functools.partial(_arrange_hubs, ax_name="tensor")
 
 
 def apply_layer_norm(input_row_block, norm_gain, norm_bias):
@@ -243,7 +252,7 @@
     active_full, gelu_back = jax.vjp(exact_gelu, hidden)
     active = active_full.astype(jnp.bfloat16)
     mlp_part = jnp.dot(active, down_weight, preferred_element_type=jnp.float32)
-    result = middle_state + lax.psum(mlp_part, "tensor") + down_bias.astype(jnp.float32)
+    result = middle_state + put_group(mlp_part) + down_bias.astype(jnp.float32)
     block_output = result.astype(jnp.bfloat16)
     output_gradient = (
         cotangent.astype(jnp.float32) * valid_flags.astype(jnp.float32)[:, None, None]

time: 785 us -> 864 us (1.10)
  waiting for transfers between devices: 482 us -> 561 us
    all_gather x0 -> x1, waiting for transfers between devices: none -> 167 us  [_arrange_hubs(): passed = lax.all_gather(vals, ax_name)]
    psum x1, waiting for transfers between devices: 152 us -> 73.1 us  [per_device(): first_normed_gradient = lax.psum(back_one, 'tensor')]
    psum x1, waiting for transfers between devices: 90.8 us -> 81.5 us  [per_device(): second_normed_gradient = lax.psum(against(hidden_low, up_weight), 'tensor')]
    unnamed x126 -> x124, local copies, waits for them, and re-layouts: 20.7 us -> 15.3 us
  transfers between devices with their start and end apart: 7 -> 8, of which waited for: 6 -> 7; matrix products, arithmetic and copies ran while one was open for 7% -> 7% of each run, Pallas kernels for 0% -> 0%
where the time goes in v1:
time: 864 us; the launch traced here: 856 us
  waiting for transfers between devices  561 us (65%)
  blocking collectives  119 us (14%)
  matrix products  65.8 us (8%)
  other arithmetic  62.9 us (7%)
  between operations  25.5 us (3%)
  local copies, waits for them, and re-layouts  21.6 us (2%)
    all_gather x1, waiting for transfers between devices, _arrange_hubs(): passed = lax.all_gather(vals, ax_name)  167 us
    psum x1, waiting for transfers between devices, per_device(): lax.psum((grads[0], grads[1], grads[2], grads[3], grads[4], grads[5], gra...  133 us
    psum x1, waiting for transfers between devices, per_device(): second_normed_gradient = lax.psum(against(hidden_low, up_weight), 'tensor')  81.5 us
    psum x1, waiting for transfers between devices, per_device(): first_normed_gradient = lax.psum(back_one, 'tensor')  73.1 us
    psum x1, waiting for transfers between devices, per_device(): lax.psum(attn_part, 'tensor')  59.8 us
    psum x1, blocking collectives, per_device(): lax.psum((grads[0], grads[1], grads[2], grads[3], grads[4], grads[5], gra...  26.5 us
    all_gather x1, waiting for transfers between devices, per_device(): lax.all_gather(rounded[8], 'dp', axis=0, tiled=True)  26.4 us
    all_gather x1, waiting for transfers between devices, per_device(): lax.all_gather(rounded[10], 'dp', axis=1, tiled=True)  20.3 us
  transfers between devices with their start and end apart: 8, of which 7 were waited for; matrix products, arithmetic and copies ran while one was open for 7% of the time, Pallas kernels for 0%

profile of v1, /device:TPU:0, one launch (start us, length us, event | category | flops | bytes accessed | tf_op | source)
XLA Modules:
  0.0 856.3 jit_solution(12178948492963406852)
XLA Ops:
  7.3 1.8 convert_element_type.208
  9.8 10.3 %all-gather.2 = bf16[8,1,128]{2,1,0:T(2,128)(2,1)S(1)} all-gather(bf16[1,1,128]{2,1,0:T(2,128)(2,1)S(1)} %convert_bitcast_fusion.5), channel_id=1, replica_groups=mesh['dp'=8,'tensor'=4] {'dp'}, dimensions={0}, use_global_device_ids=true | all-gather | bytes 2304 | tf_op jit(solution)/shard_map/all_gather | solution.py:213
  20.7 8.8 %all-gather.1 = bf16[8,1,128]{2,1,0:T(2,128)(2,1)S(1)} all-gather(bf16[1,1,128]{2,1,0:T(2,128)(2,1)S(1)} %convert_bitcast_fusion.6), channel_id=1, replica_groups=mesh['dp'=8,'tensor'=4] {'dp'}, dimensions={0}, use_global_device_ids=true | all-gather | bytes 2304 | tf_op jit(solution)/shard_map/all_gather | solution.py:212
  30.3 8.1 all_gather.45
  39.5 10.1 %all_gather.46 = bf16[256,1024]{1,0:T(8,128)(2,1)S(1)} all-gather(bf16[256,128]{1,0:T(8,128)(2,1)S(1)} %convert_element_type.217), channel_id=1, replica_groups=mesh['dp'=8,'tensor'=4] {'dp'}, dimensions={1}, use_global_device_ids=true | all-gather | bytes 589824 | tf_op jit(solution)/shard_map/all_gather | solution.py:216
  50.4 2.8 convolution_bitcast_fusion.3
  57.9 3.9 convolution_convert_fusion.1
  61.8 1.9 fusion.93
  65.6 7.9 all_gather.51
  73.7 8.8 %all-gather.3 = bf16[8,1,128]{2,1,0:T(2,128)(2,1)S(1)} all-gather(bf16[1,1,128]{2,1,0:T(2,128)(2,1)S(1)} %convert_bitcast_fusion.4), channel_id=1, replica_groups=mesh['dp'=8,'tensor'=4] {'dp'}, dimensions={0}, use_global_device_ids=true | all-gather | bytes 2304 | tf_op jit(solution)/shard_map/all_gather | solution.py:217
  82.5 7.8 all-gather.5
  90.3 9.2 %all-gather.4 = bf16[8,1,128]{2,1,0:T(2,128)(2,1)S(1)} all-gather(bf16[1,1,128]{2,1,0:T(2,128)(2,1)S(1)} %convert_bitcast_fusion.3), channel_id=1, replica_groups=mesh['dp'=8,'tensor'=4] {'dp'}, dimensions={0}, use_global_device_ids=true | all-gather | bytes 2304 | tf_op jit(solution)/shard_map/all_gather | solution.py:218
  100.2 59.8 %all-reduce.7.cloned.1.call-done = f32[577,1024]{1,0:T(8,128)} async-done(((f32[577,1024]{1,0:T(8,128)}), f32[577,1024]{1,0:T(8,128)}) %all-reduce.7.cloned.1.call-update) | async-done | bytes 2363408 | tf_op jit(solution)/shard_map/psum | solution.py:244
  160.0 2.4 fusion.88
  162.8 26.4 %all-gather.15.cloned.1.call-done = bf16[1024,1024]{1,0:T(8,128)(2,1)} async-done(((bf16[128,1024]{1,0:T(8,128)(2,1)}), bf16[1024,1024]{1,0:T(8,128)(2,1)}) %all-gather.15.cloned.1.call-update) | async-done | bytes 2097168 | tf_op jit(solution)/shard_map/all_gather | solution.py:220
  189.3 10.2 %multiply_convert_fusion.1 = (bf16[577,1024]{1,0:T(8,128)(2,1)}, f32[577,1024]{1,0:T(8,128)}, f32[577,1024]{1,0:T(8,128)}) fusion(f32[1024]{0:T(1024)S(1)} %reshape.236, bf16[1024,1024]{1,0:T(8,128)(2,1)} %all-gather.15.cloned.1.call-done, f32[577,1024]{1,0:T(8,128)S(1)} %get-tuple-element.424, f32[1024]{0:T(1024)S(1)} %bitcast.161, ...), kind=kOutput, calls=%fused_computation.39 | convolution fusion | flops 1252006912 | bytes 10385928 | tf_op jit(solution)/shard_map/dot_general | solution.py:249
  199.4 20.3 %all-gather.17.cloned.1.call-done = bf16[1024,1024]{1,0:T(8,128)(2,1)} async-done(((bf16[1024,128]{1,0:T(8,128)(2,1)}), bf16[1024,1024]{1,0:T(8,128)(2,1)}) %all-gather.17.cloned.1.call-update) | async-done | bytes 2097168 | tf_op jit(solution)/shard_map/all_gather | solution.py:222
  219.7 5.7 fusion.92
  226.5 2.9 fusion.37
  229.5 4.8 convolution_bitcast_fusion.2
  235.0 8.9 %all-gather.7 = bf16[8,1,128]{2,1,0:T(2,128)(2,1)S(1)} all-gather(bf16[1,1,128]{2,1,0:T(2,128)(2,1)S(1)} %convert_bitcast_fusion.1), channel_id=1, replica_groups=mesh['dp'=8,'tensor'=4] {'dp'}, dimensions={0}, use_global_device_ids=true | all-gather | bytes 2304 | tf_op jit(solution)/shard_map/all_gather | solution.py:223
  243.9 81.5 %all-reduce.9.cloned.1.call-done = f32[577,1024]{1,0:T(8,128)} async-done(((f32[577,1024]{1,0:T(8,128)}), f32[577,1024]{1,0:T(8,128)}) %all-reduce.9.cloned.1.call-update) | async-done | bytes 2363408 | tf_op jit(solution)/shard_map/psum | solution.py:268
  325.4 2.6 multiply_reduce_fusion.5
  328.0 166.7 %all-gather.19.cloned.1.call-done = f32[4,577,1024]{2,1,0:T(8,128)} async-done(((f32[1,577,1024]{2,1,0:T(8,128)}), f32[4,577,1024]{2,1,0:T(8,128)}) %all-gather.19.cloned.1.call-update) | async-done | bytes 9453584 | tf_op jit(solution)/shard_map/all_gather | solution.py:16
  494.7 6.5 reduce_sum.295
  501.2 4.9 fusion.86
  507.4 1.9 copy.206
  509.3 4.8 convert_reduce_fusion.1
  514.1 4.4 multiply_reduce_fusion
  520.0 1.7 fusion.27
  524.4 1.8 copy.210
  526.3 4.1 convolution_bitcast_fusion.1
  530.7 5.6 fusion.30
  536.3 4.1 fusion.35
  541.9 3.5 convolution_bitcast_fusion
  547.7 1.9 copy.214
  551.4 73.1 %all-reduce.11.cloned.1.call-done = f32[577,1024]{1,0:T(8,128)} async-done(((f32[577,1024]{1,0:T(8,128)}), f32[577,1024]{1,0:T(8,128)}) %all-reduce.11.cloned.1.call-update) | async-done | bytes 2363408 | tf_op jit(solution)/shard_map/psum | solution.py:296
  624.5 3.0 fusion.16
  627.6 26.5 %all-reduce = (f32[1024]{0:T(1024)S(1)}, f32[1024]{0:T(1024)S(1)}, f32[2,4,64]{2,1,0:T(4,128)S(1)}, f32[1024]{0:T(1024)S(1)}, f32[1024]{0:T(1024)S(1)}, /*index=...) all-reduce(f32[1024]{0:T(1024)S(1)} %get-tuple-element.353, ...), channel_id=1, replica_groups=mesh['dp'=8,'tensor'=4] {'dp'}, use_global_device_ids=true, to_apply=%region_16.17 | all-reduce | flops 7680 | bytes 61440 | tf_op jit(solution)/shard_map/psum | solution.py:316
  662.8 4.8 fusion.15
  667.6 133.4 %all-reduce.13.cloned.1.call-done = (f32[3,1024,256]{1,2,0:T(8,128)}, f32[256,1024]{1,0:T(8,128)}, f32[1024,1024]{1,0:T(8,128)}, f32[1024,1024]{1,0:T(8,128)}) async-done(((f32[3,1024,256]{1,2,0:T(8,128)}, f32[256,1024]{1,0:T(8,128)}, f32[1024,1024]{1,0:T(8,128)}, f32[1024,1024]{1,0:T(8,128)}), (f32[3,1024,256]{1,2,0:T(8,128)}, f32[256,1024]{1,0:T(8,128)}, f32[1024,1024]{1,0:T(8,128)}, ...) | async-done | bytes 12582928 | tf_op jit(solution)/shard_map/psum | solution.py:316
  801.0 3.5 multiply_reduce_fusion.4
  804.4 2.2 multiply_reduce_fusion.10
  813.9 3.8 copy.218
  817.8 12.2 %psum.127 = f32[]{:T(128)} all-reduce(f32[]{:T(128)S(6)} %add.419), channel_id=1, replica_groups=mesh['dp'=8,'tensor'=4] {'tensor'}, use_global_device_ids=true, to_apply=%region_48.49 | all-reduce | flops 1 | bytes 8 | tf_op jit(solution)/shard_map/psum | solution.py:333
  837.3 1.8 fusion.76
  841.0 2.5 fusion.68
  844.9 2.5 fusion.64
  (210 shorter events, 42.5 us)
Async XLA Ops:
  7.2 42.4 %copy-start.3 = (bf16[1,577,1024]{2,1,0:T(8,128)(2,1)S(1)}, bf16[1,577,1024]{2,1,0:T(8,128)(2,1)}, u32[]{:S(2)}) copy-start(bf16[1,577,1024]{2,1,0:T(8,128)(2,1)} %param.39) | copy-start | bytes 3545092
  7.3 43.2 %all-gather.13.cloned.1.call-start = ((), (), s32[]{:S(2)}) async-start(), calls=%async_computation | async-start | bytes 1769472 | tf_op jit(solution)/shard_map/all_gather | solution.py:214
  9.1 150.9 %all-reduce.7.cloned.1.call-start = ((), (), s32[]{:S(2)}) async-start(), calls=%async_computation.1 | async-start | bytes 4784128 | tf_op jit(solution)/shard_map/psum | solution.py:244
  49.7 12.2 %copy-start.10 = (bf16[256,1024]{1,0:T(8,128)(2,1)}, bf16[256,1024]{1,0:T(8,128)(2,1)S(1)}, u32[]{:S(2)}) copy-start(bf16[256,1024]{1,0:T(8,128)(2,1)S(1)} %all_gather.46) | copy-start | bytes 1572868
  63.8 10.0 %copy-start.41 = (f32[128]{0:T(128)S(1)}, f32[128]{0:T(128)}, u32[]{:S(2)}) copy-start(f32[128]{0:T(128)} %param.47) | copy-start | bytes 1540
  63.8 18.7 %copy-start.47 = (f32[128]{0:T(128)S(1)}, f32[128]{0:T(128)}, u32[]{:S(2)}) copy-start(f32[128]{0:T(128)} %param.49) | copy-start | bytes 1540
  63.8 26.6 %copy-start.44 = (f32[128]{0:T(128)S(1)}, f32[128]{0:T(128)}, u32[]{:S(2)}) copy-start(f32[128]{0:T(128)} %param.48) | copy-start | bytes 1540
  63.8 125.4 %all-gather.15.cloned.1.call-start = ((), (), s32[]{:S(2)}) async-start(), calls=%async_computation.2 | async-start | bytes 2359296 | tf_op jit(solution)/shard_map/all_gather | solution.py:220
  64.6 155.1 %all-gather.17.cloned.1.call-start = ((), (), s32[]{:S(2)}) async-start(), calls=%async_computation.3 | async-start | bytes 2359296 | tf_op jit(solution)/shard_map/all_gather | solution.py:222
  65.6 259.8 %all-reduce.9.cloned.1.call-start = ((), (), s32[]{:S(2)}) async-start(), calls=%async_computation.4 | async-start | bytes 4784128 | tf_op jit(solution)/shard_map/psum | solution.py:268
  162.4 163.0 %copy-start.1 = (f32[577,1024]{1,0:T(8,128)}, f32[577,1024]{1,0:T(8,128)S(1)}, u32[]{:S(2)}) copy-start(f32[577,1024]{1,0:T(8,128)S(1)} %get-tuple-element.424) | copy-start | bytes 7090180
  219.7 6.9 copy-start.53
  229.4 265.2 %all-gather.19.cloned.1.call-start = ((), (), s32[]{:S(2)}) async-start(), calls=%async_computation.6 | async-start | bytes 11960320 | tf_op jit(solution)/shard_map/all_gather | solution.py:16
  234.3 390.2 %all-reduce.11.cloned.1.call-start = ((), (), s32[]{:S(2)}) async-start(), calls=%async_computation.5 | async-start | bytes 4784128 | tf_op jit(solution)/shard_map/psum | solution.py:296
  501.2 4.9 copy-start.11
  509.3 4.8 copy-start.12
  509.3 9.3 %slice-start = ((s8[5980160]{0:T(1024)(128)(4,1)}), s8[4194304]{0:T(1024)(128)(4,1)S(1)}, s32[]{:S(2)}) async-start(s8[5980160]{0:T(1024)(128)(4,1)} %bitcast.130), calls=%async_computation.8 | async-start | bytes 8388608
  530.4 270.5 %all-reduce.13.cloned.1.call-start = ((), (), s32[]{:S(2)}) async-start(), calls=%async_computation.7 | async-start | bytes 25165824 | tf_op jit(solution)/shard_map/psum | solution.py:316
  530.7 5.6 copy-start.2
  530.7 5.6 copy-start.55
  801.0 5.7 copy-start.9
  808.3 5.6 copy-start.5
  830.7 5.3 copy-start.35
  830.7 5.3 copy-start.36
  830.7 5.3 copy-start.37
  830.7 5.9 copy-start.38
  830.7 5.9 copy-start.39
  830.7 5.8 copy-start.40
  830.8 6.5 copy-start.25
  830.8 6.4 copy-start.27
  832.3 4.9 copy-start.28
  832.3 6.9 copy-start.42
  832.3 6.9 copy-start.43
  832.3 7.5 copy-start.45
  832.3 7.5 copy-start.46
  832.3 8.1 copy-start.48
  832.3 8.1 copy-start.49
  832.4 8.7 %copy-start.16 = (f32[128,1024]{1,0:T(8,128)S(1)}, f32[128,1024]{1,0:T(8,128)}, u32[]{:S(2)}) copy-start(f32[128,1024]{1,0:T(8,128)} %param.50) | copy-start | bytes 1572868
  832.4 8.6 %copy-start.21 = (f32[128,1024]{1,0:T(8,128)S(1)}, f32[128,1024]{1,0:T(8,128)}, u32[]{:S(2)}) copy-start(f32[128,1024]{1,0:T(8,128)} %param.74) | copy-start | bytes 1572868
  832.4 8.6 %copy-start.22 = (f32[128,1024]{1,0:T(8,128)S(1)}, f32[128,1024]{1,0:T(8,128)}, u32[]{:S(2)}) copy-start(f32[128,1024]{1,0:T(8,128)} %param.62) | copy-start | bytes 1572868
  837.2 6.3 copy-start.29
  837.2 6.3 copy-start.31
  837.2 6.3 copy-start.32
  837.3 7.0 copy-start.33
  837.3 7.0 copy-start.34
  837.3 7.6 copy-start.18
  837.3 7.6 copy-start.23
  837.3 7.6 copy-start.24
  (18 other events, 36.8 us)
Sparse Core Ops, SparseCore 0:
  10.5 28.3 all-gather.12
  63.9 96.0 all-reduce.6
  162.5 26.7 all-gather.14
  191.6 28.0 all-gather.16
  229.6 95.7 all-reduce.8
  326.8 167.8 all-gather.18
  530.5 93.9 all-reduce.10
  629.1 171.8 all-reduce.12
